TPU v7x, 32 devices: a whole 2x2x4 slice. The times are simulated.
32 devices in a mesh: ctx: 16 (over z, y, x), head: 2 (over core).
Axes of the slice: x: 2, y: 2, z: 4, core: 2. Of those that a mesh axis runs over, the one named last changes fastest.
Arguments:
- queries: bfloat16 [8192, 2048], P('ctx', 'head'), may hold values from -24 to 24
- keys: bfloat16 [8192, 2048], P('ctx', 'head'), may hold values from -24 to 24
- values: bfloat16 [8192, 2048], P('ctx', 'head'), may hold values from -6 to 6
- prefix_keys: bfloat16 [8192, 2048], P('ctx', 'head'), may hold values from -6 to 6
- prefix_values: bfloat16 [8192, 2048], P('ctx', 'head'), may hold values from -6 to 6
- selected: int32 [2, 64, 8, 3], P('head', 'ctx'), may hold values from 0 to 15, all different within a row; in each aligned block of 32 rows (0 to 31, 32 to 63, ..., all dimensions but the last counted through in order) at most 6 rows name the same one
- out_weight: bfloat16 [2, 1024, 4096], P('head', 'ctx'), may hold values from -0.125 to 0.125
Outputs:
- mixed: bfloat16 [8192, 4096], P('ctx', 'head')
Inputs may be any that keep to these rules, and one draw needn't show every extreme that they name: `selected`: for every head group, tile and head, 3 different prefix blocks. Among the 32 rows of one device (one head group, that device's tiles), no block is named more than 6 times.
All inputs are finite; a program needn't handle non-finite values.
Results may differ from a plain program's by a relative error of at most 0.0056.
Values may be sent and summed in bfloat16 or wider, within the bound.
No kernel may reach another device: no remote copies, remote signals or barrier semaphores. Data moves between devices by JAX's collectives and lax.ppermute only.
A program may use at most 128 MiB of HBM per device.

v0:
```python
import jax
import jax.numpy as jnp
from jax import lax
from jax.sharding import PartitionSpec as P

D_HEAD = 128
TILE = 128
BLOCK = 512
TOPK = 3


def own_attention(queries, keys, values, head_count):
    tok_rows = queries.shape[0]
    blocks_here = tok_rows // BLOCK
    per_block = BLOCK // TILE
    tile_count = blocks_here * per_block
    shaped_query = queries.reshape(blocks_here, BLOCK, head_count, D_HEAD)
    shaped_key = keys.reshape(blocks_here, BLOCK, head_count, D_HEAD)
    shaped_value = values.reshape(blocks_here, BLOCK, head_count, D_HEAD)
    scores = jnp.einsum(
        "bqhd,bkhd->bhqk", shaped_query, shaped_key, preferred_element_type=jnp.float32
    ) * D_HEAD ** (-0.5)
    visible = jnp.arange(BLOCK)[None, :] <= jnp.arange(BLOCK)[:, None]
    scores = jnp.where(visible, scores, -jnp.inf)
    row_max = jnp.max(scores, axis=3)
    weights = jnp.exp(scores - row_max[..., None])
    row_sum = jnp.sum(weights, axis=3)
    partial_out = jnp.einsum(
        "bhqk,bkhd->bhqd",
        weights.astype(jnp.bfloat16),
        shaped_value,
        preferred_element_type=jnp.float32,
    )
    partial_out = partial_out.reshape(blocks_here, head_count, per_block, TILE, D_HEAD).transpose(
        0, 2, 1, 3, 4
    )
    partial_out = partial_out.reshape(tile_count, head_count, TILE, D_HEAD)
    row_max = (
        row_max.reshape(blocks_here, head_count, per_block, TILE)
        .transpose(0, 2, 1, 3)
        .reshape(tile_count, head_count, TILE)
    )
    row_sum = (
        row_sum.reshape(blocks_here, head_count, per_block, TILE)
        .transpose(0, 2, 1, 3)
        .reshape(tile_count, head_count, TILE)
    )
    return (partial_out, row_max, row_sum)


def attend_slot(query_tile, pair_index, key_table, value_table):
    key_block = key_table[pair_index]
    value_block = value_table[pair_index]
    scores = jnp.einsum(
        "qd,kd->qk", query_tile, key_block, preferred_element_type=jnp.float32
    ) * D_HEAD ** (-0.5)
    row_max = jnp.max(scores, axis=1)
    weights = jnp.exp(scores - row_max[:, None])
    row_sum = jnp.sum(weights, axis=1)
    partial_out = jnp.dot(
        weights.astype(jnp.bfloat16), value_block, preferred_element_type=jnp.float32
    )
    return (partial_out, row_max, row_sum)


def serve_slots(query_slots, pair_slots, key_table, value_table):
    leading = pair_slots.shape
    flat_query = query_slots.reshape((-1,) + query_slots.shape[-2:])
    flat_pairs = pair_slots.reshape(-1)

    def attend_item(slot_item):
        return attend_slot(slot_item[0], slot_item[1], key_table, value_table)

    results = lax.map(attend_item, (flat_query, flat_pairs), batch_size=16)
    return tuple((result_part.reshape(leading + result_part.shape[1:]) for result_part in results))


def shards(queries, keys, values, prefix_keys, prefix_values, selected, out_weight):
    tok_rows, width_local = queries.shape
    head_count = width_local // D_HEAD
    tile_count = tok_rows // TILE
    blocks_here = tok_rows // BLOCK
    peer_count = lax.axis_size("ctx")
    block_total = peer_count * blocks_here
    request_count = tile_count * head_count * TOPK
    capacity = (request_count + block_total - 1) // block_total
    slot_count = capacity * blocks_here
    slot_total = peer_count * slot_count
    picked_ids = selected.reshape(request_count)
    owners = picked_ids // blocks_here
    local_block = picked_ids % blocks_here
    owner_onehot = (owners[:, None] == jnp.arange(peer_count, dtype=jnp.int32)[None, :]).astype(
        jnp.int32
    )
    ranking = jnp.sum((jnp.cumsum(owner_onehot, axis=0) - owner_onehot) * owner_onehot, axis=1)
    slot_of = owners * slot_count + ranking
    request_ids = jnp.arange(request_count, dtype=jnp.int32)
    matches = slot_of[None, :] == jnp.arange(slot_total, dtype=jnp.int32)[:, None]
    filled = jnp.any(matches, axis=1)
    source_of = jnp.sum(jnp.where(matches, request_ids[None, :], 0), axis=1)
    pair_of = local_block * head_count + request_ids // TOPK % head_count
    pair_slots = jnp.sum(jnp.where(matches, pair_of[None, :], 0), axis=1).reshape(
        peer_count, slot_count
    )
    tile_queries = queries.reshape(tile_count, TILE, head_count, D_HEAD).transpose(0, 2, 1, 3)
    tile_queries = tile_queries.reshape(tile_count * head_count, TILE, D_HEAD)
    outgoing = jnp.take(tile_queries, source_of // TOPK, axis=0)
    outgoing = jnp.where(filled[:, None, None], outgoing, jnp.zeros_like(outgoing))
    outgoing = outgoing.reshape(peer_count, slot_count, TILE, D_HEAD)
    key_table = prefix_keys.reshape(blocks_here, BLOCK, head_count, D_HEAD).transpose(0, 2, 1, 3)
    key_table = key_table.reshape(blocks_here * head_count, BLOCK, D_HEAD)
    value_table = prefix_values.reshape(blocks_here, BLOCK, head_count, D_HEAD).transpose(
        0, 2, 1, 3
    )
    value_table = value_table.reshape(blocks_here * head_count, BLOCK, D_HEAD)
    answers = serve_slots(
        lax.all_to_all(outgoing, "ctx", split_axis=0, concat_axis=0, tiled=True),
        lax.all_to_all(pair_slots, "ctx", split_axis=0, concat_axis=0, tiled=True),
        key_table,
        value_table,
    )
    back_out = lax.all_to_all(answers[0], "ctx", split_axis=0, concat_axis=0, tiled=True)
    back_max = lax.all_to_all(answers[1], "ctx", split_axis=0, concat_axis=0, tiled=True)
    back_sum = lax.all_to_all(answers[2], "ctx", split_axis=0, concat_axis=0, tiled=True)
    own_parts = own_attention(queries, keys, values, head_count)
    own_out, own_max, own_sum = own_parts
    sel_out = jnp.take(back_out.reshape(slot_total, TILE, D_HEAD), slot_of, axis=0)
    sel_out = sel_out.reshape(tile_count, head_count, TOPK, TILE, D_HEAD)
    sel_max = jnp.take(back_max.reshape(slot_total, TILE), slot_of, axis=0).reshape(
        tile_count, head_count, TOPK, TILE
    )
    sel_sum = jnp.take(back_sum.reshape(slot_total, TILE), slot_of, axis=0).reshape(
        tile_count, head_count, TOPK, TILE
    )
    highest = jnp.maximum(own_max, jnp.max(sel_max, axis=2))
    own_factor = jnp.exp(own_max - highest)
    sel_factor = jnp.exp(sel_max - highest[:, :, None, :])
    numerator = own_factor[..., None] * own_out + jnp.sum(sel_factor[..., None] * sel_out, axis=2)
    denominator = own_factor * own_sum + jnp.sum(sel_factor * sel_sum, axis=2)
    attention = (
        (numerator / denominator[..., None]).transpose(0, 2, 1, 3).reshape(tok_rows, width_local)
    )
    attention = attention.astype(jnp.bfloat16)
    mixed_part = jnp.dot(
        attention,
        lax.all_gather(out_weight, "ctx", axis=1, tiled=True)[0],
        preferred_element_type=jnp.float32,
    )
    return lax.psum_scatter(mixed_part, "head", scatter_dimension=1, tiled=True).astype(
        jnp.bfloat16
    )


def solution(mesh):
    return jax.shard_map(
        shards,
        mesh=mesh,
        in_specs=(
            P("ctx", "head"),
            P("ctx", "head"),
            P("ctx", "head"),
            P("ctx", "head"),
            P("ctx", "head"),
            P("head", "ctx", None, None),
            P("head", "ctx", None),
        ),
        out_specs=P("ctx", "head"),
        check_vma=False,
    )
```

profile of v0, /device:TPU:0, one launch (start us, length us, event | category | flops | bytes accessed | tf_op | source)
XLA Modules:
  0.0 428.0 jit_solution(26307148780716345)
XLA Ops:
  8.8 8.3 %all-to-all-start.1 = ((s32[16,1,6]{2,1,0:T(1,128)}), s32[16,1,6]{2,1,0:T(1,128)S(1)}, u32[]{:S(2)}, u32[]{:S(2)}) async-start(s32[16,1,6]{2,1,0:T(1,128)} %bitcast.15), calls=%async_computation.1 | async-start | bytes 16384 | tf_op jit(solution)/shard_map/all_to_all | solution.py:118
  19.4 2.7 gather_fusion.2
  22.1 3.3 select_select_fusion
  25.4 7.1 %all-to-all-start = ((bf16[16,6,128,128]{3,2,1,0:T(8,128)(2,1)}), bf16[16,6,128,128]{3,2,1,0:T(8,128)(2,1)}, u32[]{:S(2)}, u32[]{:S(2)}) async-start(bf16[16,6,128,128]{3,2,1,0:T(8,128)(2,1)} %select_select_fusion), calls=%async_computation | async-start | bytes 6291456 | tf_op jit(solution)/shard_map/all_to_all | solution.py:117
  37.1 87.8 %all-to-all-done = bf16[16,6,128,128]{3,2,1,0:T(8,128)(2,1)} async-done(((bf16[16,6,128,128]{3,2,1,0:T(8,128)(2,1)}), bf16[16,6,128,128]{3,2,1,0:T(8,128)(2,1)}, u32[]{:S(2)}, u32[]{:S(2)}) %all-to-all-start) | async-done | bytes 3145760 | tf_op jit(solution)/shard_map/all_to_all | solution.py:117
  124.9 79.1 %while.14 = (s32[]{:T(128)}, f32[6,16,128,128]{3,2,1,0:T(8,128)}, f32[6,16,128]{2,1,0:T(8,128)S(1)}, f32[6,16,128]{2,1,0:T(8,128)S(1)}, bf16[6,16,128,128]{3,2,1...) while((s32[]{:T(128)}, f32[6,16,128,128]{3,2,1,0:T(8,128)}, ...), condition=%wide.region_9.10_spmd, body=%wide.region_6.9_spmd.sunk | while | flops 545255552 | bytes 43583104 | solution.py:74
  128.7 2.0 copy-done.1
  133.9 4.2 fusion.67
  140.1 2.0 multiply_reduce_fusion.4
  142.0 2.0 copy-done.1
  147.2 4.1 fusion.67
  151.4 1.9 gather_fusion.1
  155.2 2.0 copy-done.1
  158.5 1.9 gather_fusion
  160.4 4.1 fusion.67
  168.3 2.0 copy-done.1
  173.5 4.2 fusion.67
  181.5 2.0 copy-done.1
  186.7 4.2 fusion.67
  194.7 2.0 copy-done.1
  199.9 4.1 fusion.67
  204.6 16.5 %all-to-all-start.4 = ((f32[16,6,128]{2,1,0:T(8,128)}), f32[16,6,128]{2,1,0:T(8,128)S(1)}, u32[]{:S(2)}, u32[]{:S(2)}) async-start(f32[16,6,128]{2,1,0:T(8,128)} %reshape_reshape.19), calls=%async_computation.4 | async-start | bytes 131072 | tf_op jit(solution)/shard_map/all_to_all | solution.py:124
  221.2 7.5 %all-to-all-done.4 = f32[16,6,128]{2,1,0:T(8,128)S(1)} async-done(((f32[16,6,128]{2,1,0:T(8,128)}), f32[16,6,128]{2,1,0:T(8,128)S(1)}, u32[]{:S(2)}, u32[]{:S(2)}) %all-to-all-start.4) | async-done | bytes 49184 | tf_op jit(solution)/shard_map/all_to_all | solution.py:124
  228.7 10.1 %all_to_all.29 = f32[16,6,128]{2,1,0:T(8,128)S(1)} all-to-all(f32[16,6,128]{2,1,0:T(8,128)S(1)} %reshape_reshape.17), channel_id=1, replica_groups=mesh['ctx'=16,'head'=2] {'ctx'}, dimensions={0} | all-to-all | bytes 98304 | tf_op jit(solution)/shard_map/all_to_all | solution.py:123
  238.8 4.8 %all-to-all-start.3 = ((f32[16,6,128,128]{3,2,1,0:T(8,128)}), f32[16,6,128,128]{3,2,1,0:T(8,128)}, u32[]{:S(2)}, u32[]{:S(2)}) async-start(f32[16,6,128,128]{3,2,1,0:T(8,128)} %bitcast.159), calls=%async_computation.3 | async-start | bytes 12582912 | tf_op jit(solution)/shard_map/all_to_all | solution.py:122
  247.9 2.4 fusion.23
  251.9 104.7 %all-to-all-done.3 = f32[16,6,128,128]{3,2,1,0:T(8,128)} async-done(((f32[16,6,128,128]{3,2,1,0:T(8,128)}), f32[16,6,128,128]{3,2,1,0:T(8,128)}, u32[]{:S(2)}, u32[]{:S(2)}) %all-to-all-start.3) | async-done | bytes 6291488 | tf_op jit(solution)/shard_map/all_to_all | solution.py:122
  356.6 6.4 %gather_fusion.3 = f32[96,128,128]{2,1,0:T(8,128)} fusion(f32[96,128,128]{2,1,0:T(8,128)} %bitcast.27, s32[1024]{0:T(1024)S(1)} %pad_clamp_fusion), kind=kCustom, calls=%fused_computation.5 | custom fusion | bytes 12583296 | tf_op jit(solution)/shard_map/jit(_take)/gather | solution.py:127
  363.0 4.6 %multiply_reduce_fusion.1 = f32[4,8,128,128]{3,2,1,0:T(8,128)S(1)} fusion(f32[4,8,3,128,128]{4,3,2,1,0:T(8,128)} %bitcast.156, f32[4,8,3,128]{3,2,1,0:T(4,128)S(1)} %get-tuple-element.74, pred[4,8,3]{2,1,0:T(8,128)(4,1)S(1)} %copy.82), kind=kLoop, calls=%fused_computation.33 | loop fusion | flops 4194304 | bytes 8437856 | tf_op jit(solution)/shard_map/reduce_sum | solution.py:138
  369.6 10.1 %fusion.18 = f32[512,4096]{1,0:T(8,128)} fusion(bf16[1,1024,4096]{2,1,0:T(8,128)(2,1)} %all-gather.2.cloned.1.call-done, bf16[64,8,8,128]{3,2,1,0:T(8,128)(2,1)S(1)} %bitcast.163), kind=kOutput, calls=%fused_computation.26 | convolution fusion | flops 4294967296 | bytes 17825792 | tf_op jit(solution)/shard_map/dot_general | solution.py:144
  379.7 37.6 %reduce-scatter.2.cloned.1.call-done = f32[512,2048]{1,0:T(8,128)} async-done(((f32[512,4096]{1,0:T(8,128)}), f32[512,2048]{1,0:T(8,128)}) %reduce-scatter.2.cloned.1.call-update) | async-done | bytes 4194320 | tf_op jit(solution)/shard_map/reduce_scatter | solution.py:149
  417.3 3.8 convert_element_type.27
  (114 shorter events, 53.4 us)
Async XLA Ops:
  6.5 238.0 %copy-start = (bf16[512,1024]{1,0:T(8,128)(2,1)S(1)}, bf16[512,1024]{1,0:T(8,128)(2,1)}, u32[]{:S(2)}) copy-start(bf16[512,1024]{1,0:T(8,128)(2,1)} %param.12) | copy-start | bytes 3145732
  8.8 16.6 %all-to-all-start.1 = ((s32[16,1,6]{2,1,0:T(1,128)}), s32[16,1,6]{2,1,0:T(1,128)S(1)}, u32[]{:S(2)}, u32[]{:S(2)}) async-start(s32[16,1,6]{2,1,0:T(1,128)} %bitcast.15), calls=%async_computation.1 | async-start | bytes 16384 | tf_op jit(solution)/shard_map/all_to_all | solution.py:118
  25.4 7.9 %copy-start.2 = (bf16[512,1024]{1,0:T(8,128)(2,1)S(1)}, bf16[512,1024]{1,0:T(8,128)(2,1)}, u32[]{:S(2)}) copy-start(bf16[512,1024]{1,0:T(8,128)(2,1)} %param.14) | copy-start | bytes 3145732
  25.4 9.2 %copy-start.3 = (bf16[512,1024]{1,0:T(8,128)(2,1)S(1)}, bf16[512,1024]{1,0:T(8,128)(2,1)}, u32[]{:S(2)}) copy-start(bf16[512,1024]{1,0:T(8,128)(2,1)} %param.15) | copy-start | bytes 3145732
  25.4 99.5 %all-to-all-start = ((bf16[16,6,128,128]{3,2,1,0:T(8,128)(2,1)}), bf16[16,6,128,128]{3,2,1,0:T(8,128)(2,1)}, u32[]{:S(2)}, u32[]{:S(2)}) async-start(bf16[16,6,128,128]{3,2,1,0:T(8,128)(2,1)} %select_select_fusion), calls=%async_computation | async-start | bytes 6291456 | tf_op jit(solution)/shard_map/all_to_all | solution.py:117
  32.5 337.1 %all-gather.2.cloned.1.call-start = ((), (), s32[]{:S(2)}) async-start(), calls=%async_computation.6 | async-start | bytes 8912896 | tf_op jit(solution)/shard_map/all_gather | solution.py:146
  128.7 2.0 copy-start.1
  142.0 2.0 copy-start.1
  155.2 2.0 copy-start.1
  168.3 2.0 copy-start.1
  181.5 2.0 copy-start.1
  194.7 2.0 copy-start.1
  204.6 24.1 %all-to-all-start.4 = ((f32[16,6,128]{2,1,0:T(8,128)}), f32[16,6,128]{2,1,0:T(8,128)S(1)}, u32[]{:S(2)}, u32[]{:S(2)}) async-start(f32[16,6,128]{2,1,0:T(8,128)} %reshape_reshape.19), calls=%async_computation.4 | async-start | bytes 131072 | tf_op jit(solution)/shard_map/all_to_all | solution.py:124
  238.8 5.1 %copy-start.5 = (s32[1,4,8,3]{2,1,3,0:T(4,128)S(1)}, s32[1,4,8,3]{2,1,3,0:T(4,128)}, u32[]{:S(2)}) copy-start(s32[1,4,8,3]{2,1,3,0:T(4,128)} %param.16) | copy-start | bytes 1156
  238.8 5.7 %copy-start.4 = (bf16[512,1024]{1,0:T(8,128)(2,1)S(1)}, bf16[512,1024]{1,0:T(8,128)(2,1)}, u32[]{:S(2)}) copy-start(bf16[512,1024]{1,0:T(8,128)(2,1)} %param.11) | copy-start | bytes 3145732
  238.8 117.8 %all-to-all-start.3 = ((f32[16,6,128,128]{3,2,1,0:T(8,128)}), f32[16,6,128,128]{3,2,1,0:T(8,128)}, u32[]{:S(2)}, u32[]{:S(2)}) async-start(f32[16,6,128,128]{3,2,1,0:T(8,128)} %bitcast.159), calls=%async_computation.3 | async-start | bytes 12582912 | tf_op jit(solution)/shard_map/all_to_all | solution.py:122
  243.6 173.7 %reduce-scatter.2.cloned.1.call-start = ((), (), s32[]{:S(2)}) async-start(), calls=%async_computation.7 | async-start | bytes 12582912 | tf_op jit(solution)/shard_map/reduce_scatter | solution.py:149
  246.1 1.8 copy-start.6
Sparse Core Ops, SparseCore 0:
  36.1 155.2 all-gather.1
  379.8 37.4 reduce-scatter.1
where the time goes:
time: 430 us; the launch traced here: 428 us
  waiting for transfers between devices  238 us (55%)
  local copies, waits for them, and re-layouts  54.2 us (13%)
  matrix products  50.2 us (12%)
  starting transfers between devices  37 us (9%)
  other arithmetic  24.2 us (6%)
  between operations  13.8 us (3%)
  blocking collectives  10.1 us (2%)
    all_to_all x1, waiting for transfers between devices, shards(): lax.all_to_all(answers[0], 'ctx', split_axis=0, concat_axis=0, tiled=True)  105 us
    all_to_all x1, waiting for transfers between devices, shards(): lax.all_to_all(outgoing, 'ctx', split_axis=0, concat_axis=0, tiled=True)  87.8 us
    reduce_scatter x1, waiting for transfers between devices, shards(): lax.psum_scatter(mixed_part, 'head', scatter_dimension=1, tiled=True)  37.6 us
    dot_general x6, matrix products, attend_slot(): jnp.dot(weights.astype(jnp.bfloat16), value_block, preferred_element_type...  25 us
    all_to_all x1, starting transfers between devices, shards(): lax.all_to_all(answers[2], 'ctx', split_axis=0, concat_axis=0, tiled=True)  16.5 us
    while x12, local copies, waits for them, and re-layouts  11.8 us
    gather x6, local copies, waits for them, and re-layouts, attend_slot(): value_block = value_table[pair_index]  11.5 us
    gather x6, local copies, waits for them, and re-layouts, attend_slot(): key_block = key_table[pair_index]  11.5 us
  transfers between devices with their start and end apart: 6, of which 4 were waited for; matrix products, arithmetic and copies ran while one was open for 23% of the time, Pallas kernels for 0%

commit v1 on v0

v1 whole, which is shorter than its diff:
```python
import math

import jax
import jax.numpy as jnp
from jax import lax
from jax.experimental import pallas as pl
from jax.experimental.pallas import tpu as pltpu
from jax.sharding import PartitionSpec as P

D_HEAD = 128
TILE = 128
BLOCK = 512
TOPK = 3
SCALE = D_HEAD ** (-0.5)
LOG2E = 1.4426950408889634
BF16 = jnp.bfloat16
F32 = jnp.float32


def round_up(n, m):
    return (n + m - 1) // m * m


def smem():
    return pl.BlockSpec(memory_space=pltpu.SMEM)


def route_queries(picked, queries, peers, slots, blocks_here):
    tok_rows, width = queries.shape
    heads = width // D_HEAD
    requests = picked.shape[0]
    tail = round_up(slots, 16)
    rows = slots * TILE + tail
    steps = 4 if peers % 4 == 0 else 1
    per_step = peers // steps
    full = peers * slots == requests

    def body(picked_ref, q_ref, out_ref, owner_ref, rank_ref, source, pair, count):
        step = pl.program_id(0)

        @pl.when(step == 0)
        def _():
            for p in range(peers):
                count[p] = 0
            if not full:
                for i in range(peers * slots):
                    source[i] = -1
                    pair[i] = 0
            for r in range(requests):
                block = picked_ref[r]
                owner = block // blocks_here if blocks_here > 1 else block
                local = block % blocks_here if blocks_here > 1 else 0
                rank = count[owner]
                slot = owner * slots + rank
                source[slot] = r // TOPK
                pair[slot] = local * heads + (r // TOPK) % heads
                count[owner] = rank + 1
                owner_ref[r] = owner
                rank_ref[r] = rank

        sub = lax.broadcasted_iota(jnp.int32, (tail, TILE), 0)
        for i in range(per_step):
            ids = jnp.zeros((tail, TILE), F32)
            for s in range(slots):
                slot = (step * per_step + i) * slots + s
                row = source[slot]
                safe = row if full else jnp.maximum(row, 0)
                start = pl.multiple_of((safe // heads) * TILE, TILE)
                lane = pl.multiple_of((safe % heads) * D_HEAD, D_HEAD)
                q = q_ref[pl.ds(start, TILE), pl.ds(lane, D_HEAD)]
                if not full:
                    q = jnp.where(row >= 0, q, jnp.zeros_like(q))
                out_ref[i, s * TILE : (s + 1) * TILE, :] = q
                ids = jnp.where(sub == s, pair[slot].astype(F32), ids)
            out_ref[i, slots * TILE :, :] = ids.astype(BF16)

    return pl.pallas_call(
        body,
        grid=(steps,),
        in_specs=[smem(), pl.BlockSpec((tok_rows, width), lambda i: (0, 0))],
        out_specs=[pl.BlockSpec((per_step, rows, TILE), lambda i: (i, 0, 0)), smem(), smem()],
        out_shape=[
            jax.ShapeDtypeStruct((peers, rows, TILE), BF16),
            jax.ShapeDtypeStruct((requests,), jnp.int32),
            jax.ShapeDtypeStruct((requests,), jnp.int32),
        ],
        scratch_shapes=[
            pltpu.SMEM((peers * slots,), jnp.int32),
            pltpu.SMEM((peers * slots,), jnp.int32),
            pltpu.SMEM((peers,), jnp.int32),
        ],
        name="route",
    )(picked, queries)


def soft(scores):
    top = jnp.max(scores, axis=0, keepdims=True)
    weights = jnp.exp2((scores - top) * (SCALE * LOG2E))
    total = jnp.sum(weights, axis=0, keepdims=True)
    return weights.astype(BF16), total, top * SCALE + jnp.log(total)


def dot_nt(a, b):
    return lax.dot_general(a, b, (((1,), (1,)), ((), ())), preferred_element_type=F32)


def attend_slots(pairs, incoming, keys, values_t, slots, heads):
    peers, rows, _ = incoming.shape
    tail = round_up(3 * slots, 16)
    out_rows = slots * TILE + tail
    blocks = keys.shape[0] // BLOCK

    def body(pair_ref, q_ref, k_ref, v_ref, out_ref):
        p = pl.program_id(0)
        sub = lax.broadcasted_iota(jnp.int32, (tail, TILE), 0)
        logs = jnp.zeros((tail, TILE), F32)
        for s in range(slots):
            pair = pair_ref[p * slots + s]
            head = pair % heads if blocks > 1 else pair
            start = pl.multiple_of(pair // heads * BLOCK, BLOCK) if blocks > 1 else 0
            lane = pl.multiple_of(head * D_HEAD, D_HEAD)
            k = k_ref[pl.ds(start, BLOCK), pl.ds(lane, D_HEAD)]
            v = v_ref[pl.ds(lane, D_HEAD), pl.ds(start, BLOCK)]
            q = q_ref[0, s * TILE : (s + 1) * TILE, :]
            weights, total, lse = soft(dot_nt(k, q))
            out = jnp.dot(v, weights, preferred_element_type=F32) / total
            out_ref[0, s * TILE : (s + 1) * TILE, :] = out.astype(BF16)
            high = lse.astype(BF16).astype(F32)
            middle = (lse - high).astype(BF16).astype(F32)
            low = lse - high - middle
            logs = jnp.where(sub == 3 * s, high, logs)
            logs = jnp.where(sub == 3 * s + 1, middle, logs)
            logs = jnp.where(sub == 3 * s + 2, low, logs)
        out_ref[0, slots * TILE :, :] = logs.astype(BF16)

    return pl.pallas_call(
        body,
        grid=(peers,),
        in_specs=[
            smem(),
            pl.BlockSpec((1, rows, TILE), lambda i: (i, 0, 0)),
            pl.BlockSpec(keys.shape, lambda i: (0, 0)),
            pl.BlockSpec(values_t.shape, lambda i: (0, 0)),
        ],
        out_specs=pl.BlockSpec((1, out_rows, TILE), lambda i: (i, 0, 0)),
        out_shape=jax.ShapeDtypeStruct((peers, out_rows, TILE), BF16),
        name="attend",
    )(pairs, incoming, keys, values_t)


def own_attention(queries, keys, values_t):
    tok_rows, width = queries.shape
    heads = width // D_HEAD
    blocks = tok_rows // BLOCK

    def body(q_ref, k_ref, v_ref, out_ref, lse_ref):
        for t in range(BLOCK // TILE):
            seen = (t + 1) * TILE
            scores = dot_nt(k_ref[:seen, :], q_ref[t * TILE : seen, :])
            key = lax.broadcasted_iota(jnp.int32, scores.shape, 0)
            query = lax.broadcasted_iota(jnp.int32, scores.shape, 1) + t * TILE
            weights, total, lse = soft(jnp.where(key <= query, scores, -jnp.inf))
            out = jnp.dot(v_ref[:, :seen], weights, preferred_element_type=F32) / total
            out_ref[:, t * TILE : seen] = out
            lse_ref[0, :, t * TILE : seen] = lse

    block = pl.BlockSpec((BLOCK, D_HEAD), lambda b, h: (b, h))
    block_t = pl.BlockSpec((D_HEAD, BLOCK), lambda b, h: (h, b))
    return pl.pallas_call(
        body,
        grid=(blocks, heads),
        in_specs=[block, block, block_t],
        out_specs=[block_t, pl.BlockSpec((1, 1, BLOCK), lambda b, h: (h, 0, b))],
        out_shape=[
            jax.ShapeDtypeStruct((width, tok_rows), F32),
            jax.ShapeDtypeStruct((heads, 1, tok_rows), F32),
        ],
        name="own",
    )(queries, keys, values_t)


def combine(owner, rank, place, back, own_out, own_lse, slots):
    peers, rows, _ = back.shape
    width, tok_rows = own_out.shape
    heads = width // D_HEAD
    tiles = tok_rows // TILE
    chunk = width // peers
    tail = rows - slots * TILE

    def body(owner_ref, rank_ref, place_ref, back_ref, out_ref, lse_ref, att_ref, turned):
        t = pl.program_id(0)
        sub = lax.broadcasted_iota(jnp.int32, (tail, TILE), 0)
        for h in range(heads):
            logs, parts = [lse_ref[h]], [out_ref[h * D_HEAD : (h + 1) * D_HEAD, :]]
            for j in range(TOPK):
                r = (t * heads + h) * TOPK + j
                p, s = owner_ref[r], rank_ref[r]
                start = pl.multiple_of(s * TILE, TILE)
                parts.append(back_ref[p, pl.ds(start, TILE), :].astype(F32))
                terms = back_ref[p, slots * TILE :, :].astype(F32)
                mine = jnp.logical_and(sub >= 3 * s, sub < 3 * s + 3)
                logs.append(jnp.sum(jnp.where(mine, terms, 0.0), axis=0, keepdims=True))
            top = logs[0]
            for log in logs[1:]:
                top = jnp.maximum(top, log)
            factors = [jnp.exp(log - top) for log in logs]
            inverse = 1.0 / (factors[0] + factors[1] + factors[2] + factors[3])
            mixed = parts[0] * (factors[0] * inverse)
            for factor, part in zip(factors[1:], parts[1:]):
                mixed = mixed + part * (factor * inverse)
            for i in range(D_HEAD // chunk):
                at = pl.multiple_of(place_ref[h * (D_HEAD // chunk) + i] * chunk, chunk)
                turned[pl.ds(at, chunk), :] = mixed[i * chunk : (i + 1) * chunk, :]
        for h in range(heads):
            lanes = slice(h * D_HEAD, (h + 1) * D_HEAD)
            att_ref[:, lanes] = turned[lanes, :].T.astype(BF16)

    return pl.pallas_call(
        body,
        grid=(tiles,),
        in_specs=[
            smem(),
            smem(),
            smem(),
            pl.BlockSpec(back.shape, lambda i: (0, 0, 0)),
            pl.BlockSpec((width, TILE), lambda i: (0, i)),
            pl.BlockSpec((heads, 1, TILE), lambda i: (0, 0, i)),
        ],
        out_specs=pl.BlockSpec((TILE, width), lambda i: (i, 0)),
        out_shape=jax.ShapeDtypeStruct((tok_rows, width), BF16),
        scratch_shapes=[pltpu.VMEM((width, TILE), F32)],
        name="combine",
    )(owner, rank, place, back, own_out, own_lse)


def project(att_own, att_other, w_own, w_other):
    rows, depth = att_own.shape
    width = w_own.shape[1]
    part = min(width, 512)

    def body(a_ref, b_ref, wa_ref, wb_ref, out_ref):
        total = jnp.dot(a_ref[...], wa_ref[...], preferred_element_type=F32)
        total += jnp.dot(b_ref[...], wb_ref[...], preferred_element_type=F32)
        out_ref[...] = total.astype(BF16)

    held = pl.BlockSpec((rows, depth), lambda i: (0, 0))
    weight = pl.BlockSpec((depth, part), lambda i: (0, i))
    return pl.pallas_call(
        body,
        grid=(width // part,),
        in_specs=[held, held, weight, weight],
        out_specs=pl.BlockSpec((rows, part), lambda i: (0, i)),
        out_shape=jax.ShapeDtypeStruct((rows, width), BF16),
        name="project",
    )(att_own, att_other, w_own, w_other)


def bit_orders(peers):
    bits = int(math.log2(peers))
    high = list(range(bits - 1, 1, -1))
    return [high + [1, 0], high + [0, 1]]


def doubling_pairs(peers, orders, step, other):
    pairs = []
    for c in range(peers):
        for h in range(2):
            group = 1 - h if other else h
            pairs.append((2 * c + h, 2 * (c ^ (1 << orders[group][step])) + h))
    return pairs


def shards(queries, keys, values, prefix_keys, prefix_values, selected, out_weight):
    tok_rows, width = queries.shape
    heads = width // D_HEAD
    tiles = tok_rows // TILE
    blocks_here = prefix_keys.shape[0] // BLOCK
    peers = lax.axis_size("ctx")
    me, core = lax.axis_index("ctx"), lax.axis_index("head")
    requests = tiles * heads * TOPK
    capacity = -(-requests // (peers * blocks_here))
    slots = capacity * blocks_here
    swap = [(0, 1), (1, 0)]

    outgoing, owner, rank = route_queries(
        selected.reshape(requests), queries, peers, slots, blocks_here
    )
    incoming = lax.all_to_all(outgoing, "ctx", split_axis=0, concat_axis=0, tiled=True)

    half = out_weight.shape[2] // 2
    weight = out_weight[0]
    w_own = lax.dynamic_slice_in_dim(weight, core * half, half, 1)
    w_other = lax.ppermute(
        lax.dynamic_slice_in_dim(weight, (1 - core) * half, half, 1), "head", swap
    )
    orders = bit_orders(peers)
    for step in range(len(orders[0])):
        got = lax.ppermute(w_own, ("ctx", "head"), doubling_pairs(peers, orders, step, False))
        w_own = jnp.concatenate([w_own, got], axis=0)
        got = lax.ppermute(w_other, ("ctx", "head"), doubling_pairs(peers, orders, step, True))
        w_other = jnp.concatenate([w_other, got], axis=0)

    apart = jnp.arange(peers, dtype=jnp.int32) ^ me
    places = [sum(((apart >> bit) & 1) << k for k, bit in enumerate(order)) for order in orders]
    place = jnp.where(core == 0, places[0], places[1])

    own_out, own_lse = own_attention(queries, keys, values.T)
    pairs = incoming[:, slots * TILE : slots * TILE + slots, 0].astype(jnp.int32)
    answers = attend_slots(
        pairs.reshape(peers * slots), incoming, prefix_keys, prefix_values.T, slots, heads
    )
    back = lax.all_to_all(answers, "ctx", split_axis=0, concat_axis=0, tiled=True)
    att = combine(owner, rank, place, back, own_out, own_lse, slots)
    att_other = lax.ppermute(att, "head", swap)
    return project(att, att_other, w_own, w_other)


def solution(mesh):
    return jax.shard_map(
        shards,
        mesh=mesh,
        in_specs=(
            P("ctx", "head"),
            P("ctx", "head"),
            P("ctx", "head"),
            P("ctx", "head"),
            P("ctx", "head"),
            P("head", "ctx", None, None),
            P("head", "ctx", None),
        ),
        out_specs=P("ctx", "head"),
        check_vma=False,
    )
```

time: 430 us -> 305 us (0.71)
  waiting for transfers between devices: 238 us -> 184 us
  matrix products: 50.2 us -> 0 us
  Pallas kernels: 0 us -> 48.6 us
  local copies, waits for them, and re-layouts: 54.2 us -> 33.2 us
  other arithmetic: 24.2 us -> 4.15 us
  between operations: 13.8 us -> 0.1 us
  blocking collectives: 10.1 us -> 0 us
    ppermute x0 -> x10, waiting for transfers between devices: none -> 124 us  [the longest x4 100 us: shards(): lax.ppermute(w_own, ('ctx', 'head'), doubling_pairs(peers, orders, step,...]
    all_to_all x3 -> x1, waiting for transfers between devices: 112 us -> 0.01 us  [shards(): lax.all_to_all(answers, 'ctx', split_axis=0, concat_axis=0, tiled=True)]
    dot_general x15 -> x0, matrix products: 50.2 us -> none  [the longest x6 25 us: attend_slot(): jnp.dot(weights.astype(jnp.bfloat16), value_block, preferred_element_type...]
    pallas_call x0 -> x5, Pallas kernels: none -> 48.6 us  [the longest x1 19.9 us: attend_slots(): pl.pallas_call(body, grid=(peers,), in_specs=[smem(), pl.BlockSpec((1, ro...]
    reduce_scatter x1 -> x0, waiting for transfers between devices: 37.6 us -> none  [shards(): lax.psum_scatter(mixed_part, 'head', scatter_dimension=1, tiled=True)]
    gather x16 -> x0, local copies, waits for them, and re-layouts: 33.4 us -> none  [the longest x6 11.5 us: attend_slot(): value_block = value_table[pair_index]]
    all_to_all x1, waiting for transfers between devices: 87.8 us -> 59.7 us  [shards(): lax.all_to_all(outgoing, 'ctx', split_axis=0, concat_axis=0, tiled=True)]
    unnamed x16 -> x29, local copies, waits for them, and re-layouts: 5.05 us -> 23.7 us
  transfers between devices with their start and end apart: 6 -> 12, of which waited for: 4 -> 9; matrix products, arithmetic and copies ran while one was open for 23% -> 10% of each run, Pallas kernels for 0% -> 5%
where the time goes in v1:
time: 305 us; the launch traced here: 304 us
  waiting for transfers between devices  184 us (60%)
  Pallas kernels  48.6 us (16%)
  starting transfers between devices  34.7 us (11%)
  local copies, waits for them, and re-layouts  33.2 us (11%)
  other arithmetic  4.15 us (1%)
    ppermute x4, waiting for transfers between devices, shards(): lax.ppermute(w_own, ('ctx', 'head'), doubling_pairs(peers, orders, step,...  100 us
    all_to_all x1, waiting for transfers between devices, shards(): lax.all_to_all(outgoing, 'ctx', split_axis=0, concat_axis=0, tiled=True)  59.7 us
    unnamed x29, local copies, waits for them, and re-layouts  23.7 us
    ppermute x4, waiting for transfers between devices, shards(): lax.ppermute(w_other, ('ctx', 'head'), doubling_pairs(peers, orders, step...  23.7 us
    pallas_call x1, Pallas kernels, attend_slots(): pl.pallas_call(body, grid=(peers,), in_specs=[smem(), pl.BlockSpec((1, ro...  19.9 us
    all_to_all x1, starting transfers between devices, shards(): lax.all_to_all(answers, 'ctx', split_axis=0, concat_axis=0, tiled=True)  15.4 us
    pallas_call x1, Pallas kernels, own_attention(): pl.pallas_call(body, grid=(blocks, heads), in_specs=[block, block, block_...  9.97 us
    pallas_call x1, Pallas kernels, project(): pl.pallas_call(body, grid=(width // part,), in_specs=[held, held, weight,...  8.63 us
  transfers between devices with their start and end apart: 12, of which 9 were waited for; matrix products, arithmetic and copies ran while one was open for 10% of the time, Pallas kernels for 5%

profile of v1, /device:TPU:0, one launch (start us, length us, event | category | flops | bytes accessed | tf_op | source)
XLA Modules:
  0.0 304.3 jit_solution(12761759248428597043)
XLA Ops:
  1.4 4.4 %route.1 = (bf16[16,784,128]{2,1,0:T(8,128)(2,1)}, s32[96]{0:T(128)}, s32[96]{0:T(128)}) custom-call(s32[96]{0:T(128)} %reshape.9.picked_ref, bf16[512,1024]{1,0:T(8,128)(2,1)} %q_ref.3), custom_call_target="tpu_custom_call" | custom-call | tf_op jit(solution)/shard_map/route/pallas_call | solution.py:77
  5.8 8.3 %all-to-all-start = ((bf16[16,784,128]{2,1,0:T(8,128)(2,1)}), bf16[16,784,128]{2,1,0:T(8,128)(2,1)S(1)}, u32[]{:S(2)}, u32[]{:S(2)}) async-start(bf16[16,784,128]{2,1,0:T(8,128)(2,1)} %get-tuple-element.12), calls=%async_computation | async-start | bytes 6422528 | tf_op jit(solution)/shard_map/all_to_all | solution.py:288
  14.2 2.3 copy.12
  16.4 59.7 %all-to-all-done.q_ref = bf16[16,784,128]{2,1,0:T(8,128)(2,1)S(1)} async-done(((bf16[16,784,128]{2,1,0:T(8,128)(2,1)}), bf16[16,784,128]{2,1,0:T(8,128)(2,1)S(1)}, u32[]{:S(2)}, u32[]{:S(2)}) %all-to-all-start) | async-done | bytes 3211296 | tf_op jit(solution)/shard_map/all_to_all | solution.py:288
  77.8 19.9 %attend.1 = bf16[16,800,128]{2,1,0:T(8,128)(2,1)} custom-call(s32[96]{0:T(128)} %reshape.10.pair_ref, bf16[16,784,128]{2,1,0:T(8,128)(2,1)} %copy-done.1, bf16[512,1024]{1,0:T(8,128)(2,1)} %k_ref.2, bf16[1024,512]{1,0:T(8,128)(2,1)} %bitcast.9), custom_call_target="tpu_custom_call" | custom-call | tf_op jit(solution)/shard_map/attend/pallas_call | solution.py:136
  97.8 15.4 %all-to-all-start.1 = ((bf16[16,800,128]{2,1,0:T(8,128)(2,1)}), bf16[16,800,128]{2,1,0:T(8,128)(2,1)S(1)}, u32[]{:S(2)}, u32[]{:S(2)}) async-start(bf16[16,800,128]{2,1,0:T(8,128)(2,1)} %attend.1), calls=%async_computation.1 | async-start | bytes 6553600 | tf_op jit(solution)/shard_map/all_to_all | solution.py:312
  113.2 1.7 dynamic-slice_bitcast_fusion
  114.9 1.7 constant_dynamic-update-slice_fusion.4
  116.6 2.8 collective-permute-start.1
  119.5 84.3 %collective-permute-done.1 = bf16[64,2048]{1,0:T(8,128)(2,1)S(1)} collective-permute-done((bf16[64,2048]{1,0:T(8,128)(2,1)S(1)}, bf16[64,2048]{1,0:T(8,128)(2,1)S(1)}, u32[]{:S(2)}, u32[]{:S(2)}) %collective-permute-start.1) | collective-permute-done | bytes 262176 | tf_op jit(solution)/shard_map/ppermute | solution.py:298
  203.9 4.6 %collective-permute-done.6 = bf16[64,2048]{1,0:T(8,128)(2,1)S(1)} collective-permute-done((bf16[64,2048]{1,0:T(8,128)(2,1)S(1)}, bf16[64,2048]{1,0:T(8,128)(2,1)S(1)}, u32[]{:S(2)}, u32[]{:S(2)}) %collective-permute-start.6) | collective-permute-done | bytes 262176 | tf_op jit(solution)/shard_map/ppermute | solution.py:300
  208.6 11.1 %collective-permute-done.2 = bf16[128,2048]{1,0:T(8,128)(2,1)S(1)} collective-permute-done((bf16[128,2048]{1,0:T(8,128)(2,1)S(1)}, bf16[128,2048]{1,0:T(8,128)(2,1)S(1)}, u32[]{:S(2)}, u32[]{:S(2)}) %collective-permute-start.2) | collective-permute-done | bytes 524320 | tf_op jit(solution)/shard_map/ppermute | solution.py:298
  219.8 2.6 collective-permute-start.3
  222.4 8.5 %collective-permute-done.7 = bf16[128,2048]{1,0:T(8,128)(2,1)S(1)} collective-permute-done((bf16[128,2048]{1,0:T(8,128)(2,1)S(1)}, bf16[128,2048]{1,0:T(8,128)(2,1)S(1)}, u32[]{:S(2)}, u32[]{:S(2)}) %collective-permute-start.7) | collective-permute-done | bytes 524320 | tf_op jit(solution)/shard_map/ppermute | solution.py:300
  232.5 3.4 %collective-permute-done.3 = bf16[256,2048]{1,0:T(8,128)(2,1)S(1)} collective-permute-done((bf16[256,2048]{1,0:T(8,128)(2,1)S(1)}, bf16[256,2048]{1,0:T(8,128)(2,1)S(1)}, u32[]{:S(2)}, u32[]{:S(2)}) %collective-permute-start.3) | collective-permute-done | bytes 1048608 | tf_op jit(solution)/shard_map/ppermute | solution.py:298
  235.9 1.5 pad_maximum_fusion
  238.7 7.1 %collective-permute-done.8 = bf16[256,2048]{1,0:T(8,128)(2,1)S(1)} collective-permute-done((bf16[256,2048]{1,0:T(8,128)(2,1)S(1)}, bf16[256,2048]{1,0:T(8,128)(2,1)S(1)}, u32[]{:S(2)}, u32[]{:S(2)}) %collective-permute-start.8) | collective-permute-done | bytes 1048608 | tf_op jit(solution)/shard_map/ppermute | solution.py:300
  248.3 2.5 collective-permute-start.9
  250.8 2.3 copy.13
  253.1 10.0 %own.1 = (f32[1024,512]{1,0:T(8,128)}, f32[8,1,512]{2,1,0:T(1,128)}) custom-call(bf16[512,1024]{1,0:T(8,128)(2,1)} %q_ref.3, bf16[512,1024]{1,0:T(8,128)(2,1)} %k_ref.3, bf16[1024,512]{1,0:T(8,128)(2,1)} %bitcast.10), custom_call_target="tpu_custom_call" | custom-call | tf_op jit(solution)/shard_map/own/pallas_call | solution.py:169
  264.3 1.7 constant_dynamic-update-slice_fusion.3
  266.0 1.7 constant_dynamic-update-slice_fusion.8
  267.7 1.9 constant_dynamic-update-slice_fusion.2
  269.6 1.9 constant_dynamic-update-slice_fusion.7
  271.5 1.7 copy-done
  273.2 5.7 %combine.1.a_ref = bf16[512,1024]{1,0:T(8,128)(2,1)} custom-call(s32[96]{0:T(128)} %get-tuple-element.10.owner_ref, s32[96]{0:T(128)} %get-tuple-element.11.rank_ref, s32[16]{0:T(128)} %broadcast_select_fusion.place_ref, bf16[16,800,128]{2,1,0:T(8,128)(2,1)} %copy-done, f32[1024,512]{1,0:T(8,128)} %get-tuple-element.13.out_ref, ...), custom_call_target="tpu_custom_call" | custom-call | tf_op jit(solution)/shard_map/combine/pallas_call | solution.py:218
  278.8 2.3 constant_dynamic-update-slice_fusion.1
  281.1 2.3 constant_dynamic-update-slice_fusion.6
  284.8 3.1 %constant_dynamic-update-slice_fusion.wa_ref = bf16[1024,2048]{1,0:T(8,128)(2,1)} fusion(bf16[1024,2048]{1,0:T(8,128)(2,1)} %constant_dynamic-update-slice_fusion.1, bf16[512,2048]{1,0:T(8,128)(2,1)} %collective-permute-done.4), kind=kLoop, calls=%fused_computation.9 | loop fusion | bytes 4194304 | tf_op jit(solution)/shard_map/concatenate | solution.py:299
  288.0 3.5 %collective-permute-done.9 = bf16[512,2048]{1,0:T(8,128)(2,1)} collective-permute-done((bf16[512,2048]{1,0:T(8,128)(2,1)}, bf16[512,2048]{1,0:T(8,128)(2,1)}, u32[]{:S(2)}, u32[]{:S(2)}) %collective-permute-start.9) | collective-permute-done | bytes 2097184 | tf_op jit(solution)/shard_map/ppermute | solution.py:300
  291.4 3.2 %constant_dynamic-update-slice_fusion.5.wb_ref = bf16[1024,2048]{1,0:T(8,128)(2,1)} fusion(bf16[1024,2048]{1,0:T(8,128)(2,1)} %constant_dynamic-update-slice_fusion.6, bf16[512,2048]{1,0:T(8,128)(2,1)} %collective-permute-done.9), kind=kLoop, calls=%fused_computation.14 | loop fusion | bytes 4194304 | tf_op jit(solution)/shard_map/concatenate | solution.py:301
  295.7 8.6 %project.1 = bf16[512,2048]{1,0:T(8,128)(2,1)} custom-call(bf16[512,1024]{1,0:T(8,128)(2,1)} %combine.1.a_ref, bf16[512,1024]{1,0:T(8,128)(2,1)} %copy-done.8, bf16[1024,2048]{1,0:T(8,128)(2,1)} %constant_dynamic-update-slice_fusion.wa_ref, bf16[1024,2048]{1,0:T(8,128)(2,1)} %constant_dynamic-update-slice_fusion.5.wb_ref), custom_call_target="tpu_custom_call" | custom-call | tf_op jit(solution)/shard_map/project/pallas_call | solution.py:248
  (39 shorter events, 12.5 us)
Async XLA Ops:
  5.8 70.4 %all-to-all-start = ((bf16[16,784,128]{2,1,0:T(8,128)(2,1)}), bf16[16,784,128]{2,1,0:T(8,128)(2,1)S(1)}, u32[]{:S(2)}, u32[]{:S(2)}) async-start(bf16[16,784,128]{2,1,0:T(8,128)(2,1)} %get-tuple-element.12), calls=%async_computation | async-start | bytes 6422528 | tf_op jit(solution)/shard_map/all_to_all | solution.py:288
  76.2 1.7 copy-start.1
  97.8 173.7 %all-to-all-start.1 = ((bf16[16,800,128]{2,1,0:T(8,128)(2,1)}), bf16[16,800,128]{2,1,0:T(8,128)(2,1)S(1)}, u32[]{:S(2)}, u32[]{:S(2)}) async-start(bf16[16,800,128]{2,1,0:T(8,128)(2,1)} %attend.1), calls=%async_computation.1 | async-start | bytes 6553600 | tf_op jit(solution)/shard_map/all_to_all | solution.py:312
  114.9 4.5 %collective-permute-start.5 = (bf16[64,2048]{1,0:T(8,128)(2,1)}, bf16[64,2048]{1,0:T(8,128)(2,1)S(1)}, u32[]{:S(2)}, u32[]{:S(2)}) collective-permute-start(bf16[64,2048]{1,0:T(8,128)(2,1)} %dynamic-slice_bitcast_fusion), channel_id=1, source_target_pairs={{0,1},{1,0},{2,3},{3,2},{4,5},{5,4},{6,7},{7,6},{8,9},{9,8},{10,11... | collective-permute-start | bytes 786440 | tf_op jit(solution)/shard_map/ppermute | solution.py:293
  116.6 87.2 %collective-permute-start.1 = (bf16[64,2048]{1,0:T(8,128)(2,1)S(1)}, bf16[64,2048]{1,0:T(8,128)(2,1)S(1)}, u32[]{:S(2)}, u32[]{:S(2)}) collective-permute-start(bf16[64,2048]{1,0:T(8,128)(2,1)S(1)} %get-tuple-element.16), channel_id=1, source_target_pairs={{0,16},{1,17},{2,18},{3,19},{4,20},{5,21},{6,22},{7,23},{8,24},{9,... | collective-permute-start | bytes 786440 | tf_op jit(solution)/shard_map/ppermute | solution.py:298
  119.4 89.1 %collective-permute-start.6 = (bf16[64,2048]{1,0:T(8,128)(2,1)S(1)}, bf16[64,2048]{1,0:T(8,128)(2,1)S(1)}, u32[]{:S(2)}, u32[]{:S(2)}) collective-permute-start(bf16[64,2048]{1,0:T(8,128)(2,1)S(1)} %collective-permute-done.5), channel_id=1, source_target_pairs={{0,16},{1,17},{2,18},{3,19},{4,20},{5,21},{6,22},{7,23},{8,24},{9,... | collective-permute-start | bytes 786440 | tf_op jit(solution)/shard_map/ppermute | solution.py:300
  203.8 33.7 %copy-start.6 = (bf16[64,2048]{1,0:T(8,128)(2,1)}, bf16[64,2048]{1,0:T(8,128)(2,1)S(1)}, u32[]{:S(2)}) copy-start(bf16[64,2048]{1,0:T(8,128)(2,1)S(1)} %collective-permute-done.1) | copy-start | bytes 786436
  203.8 15.9 %collective-permute-start.2 = (bf16[128,2048]{1,0:T(8,128)(2,1)S(1)}, bf16[128,2048]{1,0:T(8,128)(2,1)S(1)}, u32[]{:S(2)}, u32[]{:S(2)}) collective-permute-start(bf16[128,2048]{1,0:T(8,128)(2,1)S(1)} %pad_maximum_fusion.4), channel_id=1, source_target_pairs={{0,8},{1,9},{2,10},{3,11},{4,12},{5,13},{6,14},{7,15},{8,0},{9,1},... | collective-permute-start | bytes 1572872 | tf_op jit(solution)/shard_map/ppermute | solution.py:298
  208.5 37.3 %copy-start.7 = (bf16[64,2048]{1,0:T(8,128)(2,1)}, bf16[64,2048]{1,0:T(8,128)(2,1)S(1)}, u32[]{:S(2)}) copy-start(bf16[64,2048]{1,0:T(8,128)(2,1)S(1)} %collective-permute-done.6) | copy-start | bytes 786436
  208.5 22.3 %collective-permute-start.7 = (bf16[128,2048]{1,0:T(8,128)(2,1)S(1)}, bf16[128,2048]{1,0:T(8,128)(2,1)S(1)}, u32[]{:S(2)}, u32[]{:S(2)}) collective-permute-start(bf16[128,2048]{1,0:T(8,128)(2,1)S(1)} %pad_maximum_fusion.5), channel_id=1, source_target_pairs={{0,8},{1,9},{2,10},{3,11},{4,12},{5,13},{6,14},{7,15},{8,0},{9,1},... | collective-permute-start | bytes 1572872 | tf_op jit(solution)/shard_map/ppermute | solution.py:300
  219.7 17.7 %copy-start.2 = (bf16[128,2048]{1,0:T(8,128)(2,1)}, bf16[128,2048]{1,0:T(8,128)(2,1)S(1)}, u32[]{:S(2)}) copy-start(bf16[128,2048]{1,0:T(8,128)(2,1)S(1)} %collective-permute-done.2) | copy-start | bytes 1572868
  219.8 16.1 %collective-permute-start.3 = (bf16[256,2048]{1,0:T(8,128)(2,1)S(1)}, bf16[256,2048]{1,0:T(8,128)(2,1)S(1)}, u32[]{:S(2)}, u32[]{:S(2)}) collective-permute-start(bf16[256,2048]{1,0:T(8,128)(2,1)S(1)} %pad_maximum_fusion.2), channel_id=1, source_target_pairs={{0,4},{1,3},{2,6},{3,1},{4,0},{5,7},{6,2},{7,5},{8,12},{9,11},{10,... | collective-permute-start | bytes 3145736 | tf_op jit(solution)/shard_map/ppermute | solution.py:298
  230.9 17.5 %copy-start.3 = (bf16[128,2048]{1,0:T(8,128)(2,1)}, bf16[128,2048]{1,0:T(8,128)(2,1)S(1)}, u32[]{:S(2)}) copy-start(bf16[128,2048]{1,0:T(8,128)(2,1)S(1)} %collective-permute-done.7) | copy-start | bytes 1572868
  231.0 14.9 %collective-permute-start.8 = (bf16[256,2048]{1,0:T(8,128)(2,1)S(1)}, bf16[256,2048]{1,0:T(8,128)(2,1)S(1)}, u32[]{:S(2)}, u32[]{:S(2)}) collective-permute-start(bf16[256,2048]{1,0:T(8,128)(2,1)S(1)} %pad_maximum_fusion.3), channel_id=1, source_target_pairs={{0,2},{1,5},{2,0},{3,7},{4,6},{5,1},{6,4},{7,3},{8,10},{9,13},{10,... | collective-permute-start | bytes 3145736 | tf_op jit(solution)/shard_map/ppermute | solution.py:300
  235.9 12.4 %copy-start.4 = (bf16[256,2048]{1,0:T(8,128)(2,1)}, bf16[256,2048]{1,0:T(8,128)(2,1)S(1)}, u32[]{:S(2)}) copy-start(bf16[256,2048]{1,0:T(8,128)(2,1)S(1)} %collective-permute-done.3) | copy-start | bytes 3145732
  237.4 47.4 %collective-permute-start.4 = (bf16[512,2048]{1,0:T(8,128)(2,1)}, bf16[512,2048]{1,0:T(8,128)(2,1)}, u32[]{:S(2)}, u32[]{:S(2)}) collective-permute-start(bf16[512,2048]{1,0:T(8,128)(2,1)} %pad_maximum_fusion), channel_id=1, source_target_pairs={{0,2},{1,5},{2,0},{3,7},{4,6},{5,1},{6,4},{7,3},{8,10},{9,13},{10,... | collective-permute-start | bytes 6291464 | tf_op jit(solution)/shard_map/ppermute | solution.py:298
  245.8 1.0 copy-start.5
  248.3 43.1 %collective-permute-start.9 = (bf16[512,2048]{1,0:T(8,128)(2,1)}, bf16[512,2048]{1,0:T(8,128)(2,1)}, u32[]{:S(2)}, u32[]{:S(2)}) collective-permute-start(bf16[512,2048]{1,0:T(8,128)(2,1)} %pad_maximum_fusion.1), channel_id=1, source_target_pairs={{0,4},{1,3},{2,6},{3,1},{4,0},{5,7},{6,2},{7,5},{8,12},{9,11},{10,... | collective-permute-start | bytes 6291464 | tf_op jit(solution)/shard_map/ppermute | solution.py:300
  271.5 1.7 copy-start
  278.8 15.8 %collective-permute-start = (bf16[512,1024]{1,0:T(8,128)(2,1)}, bf16[512,1024]{1,0:T(8,128)(2,1)S(1)}, u32[]{:S(2)}, u32[]{:S(2)}) collective-permute-start(bf16[512,1024]{1,0:T(8,128)(2,1)} %combine.1.a_ref), channel_id=1, source_target_pairs={{0,1},{1,0},{2,3},{3,2},{4,5},{5,4},{6,7},{7,6},{8,9},{9,8},{10,11... | collective-permute-start | bytes 3145736 | tf_op jit(solution)/shard_map/ppermute | solution.py:314
  294.7 1.1 copy-start.8

commit v2 on v1

v2 whole, which is shorter than its diff:
```python
import math

import jax
import jax.numpy as jnp
from jax import lax
from jax.experimental import pallas as pl
from jax.experimental.pallas import tpu as pltpu
from jax.sharding import PartitionSpec as P


D_HEAD = 128
TILE = 128
BLOCK = 512
TOPK = 3
SCALE = D_HEAD ** (-0.5)
LOG2E = 1.4426950408889634
BF16 = jnp.bfloat16
F32 = jnp.float32


def round_up(n, m):
    return (n + m - 1) // m * m


def smem():
    return pl.BlockSpec(memory_space=pltpu.SMEM)


def route_queries(picked, queries, peers, parts, blocks_here):
    tok_rows, width = queries.shape
    heads = width // D_HEAD
    requests = picked.shape[0]
    slots = sum(parts)
    tails = [round_up(n, 16) for n in parts]
    steps = 4 if peers % 4 == 0 else 1
    per_step = peers // steps
    full = peers * slots == requests

    def body(picked_ref, q_ref, *refs):
        outs, (owner_ref, rank_ref, source, pair, count) = refs[: len(parts)], refs[len(parts) :]
        step = pl.program_id(0)

        @pl.when(step == 0)
        def _():
            for p in range(peers):
                count[p] = 0
            if not full:
                for i in range(peers * slots):
                    source[i] = -1
                    pair[i] = 0
            for r in range(requests):
                block = picked_ref[r]
                owner = block // blocks_here if blocks_here > 1 else block
                local = block % blocks_here if blocks_here > 1 else 0
                rank = count[owner]
                slot = owner * slots + rank
                source[slot] = r // TOPK
                pair[slot] = local * heads + (r // TOPK) % heads
                count[owner] = rank + 1
                owner_ref[r] = owner
                rank_ref[r] = rank

        for i in range(per_step):
            first = 0
            for n, tail, out_ref in zip(parts, tails, outs):
                sub = lax.broadcasted_iota(jnp.int32, (tail, TILE), 0)
                ids = jnp.zeros((tail, TILE), F32)
                for s in range(n):
                    slot = (step * per_step + i) * slots + first + s
                    row = source[slot]
                    safe = row if full else jnp.maximum(row, 0)
                    start = pl.multiple_of((safe // heads) * TILE, TILE)
                    lane = pl.multiple_of((safe % heads) * D_HEAD, D_HEAD)
                    q = q_ref[pl.ds(start, TILE), pl.ds(lane, D_HEAD)]
                    if not full:
                        q = jnp.where(row >= 0, q, jnp.zeros_like(q))
                    out_ref[i, s * TILE : (s + 1) * TILE, :] = q
                    ids = jnp.where(sub == s, pair[slot].astype(F32), ids)
                out_ref[i, n * TILE :, :] = ids.astype(BF16)
                first += n

    rows = [n * TILE + tail for n, tail in zip(parts, tails)]
    results = pl.pallas_call(
        body,
        grid=(steps,),
        in_specs=[smem(), pl.BlockSpec((tok_rows, width), lambda i: (0, 0))],
        out_specs=[pl.BlockSpec((per_step, n, TILE), lambda i: (i, 0, 0)) for n in rows]
        + [smem(), smem()],
        out_shape=[jax.ShapeDtypeStruct((peers, n, TILE), BF16) for n in rows]
        + [jax.ShapeDtypeStruct((requests,), jnp.int32)] * 2,
        scratch_shapes=[
            pltpu.SMEM((peers * slots,), jnp.int32),
            pltpu.SMEM((peers * slots,), jnp.int32),
            pltpu.SMEM((peers,), jnp.int32),
        ],
        name="route",
    )(picked, queries)
    return results[: len(parts)], results[-2], results[-1]


def soft(scores):
    top = jnp.max(scores, axis=0, keepdims=True)
    weights = jnp.exp2((scores - top) * (SCALE * LOG2E))
    total = jnp.sum(weights, axis=0, keepdims=True)
    return weights.astype(BF16), total, top * SCALE + jnp.log(total)


def dot_nt(a, b):
    return lax.dot_general(a, b, (((1,), (1,)), ((), ())), preferred_element_type=F32)


def attend_slots(pairs, incoming, keys, values_t, slots, heads):
    peers, rows, _ = incoming.shape
    tail = round_up(3 * slots, 16)
    out_rows = slots * TILE + tail
    blocks = keys.shape[0] // BLOCK
    group = math.gcd(peers, max(1, 6 // slots))

    def body(pair_ref, q_ref, k_ref, v_ref, out_ref):
        sub = lax.broadcasted_iota(jnp.int32, (tail, TILE), 0)
        for i in range(group):
            p = pl.program_id(0) * group + i
            logs = jnp.zeros((tail, TILE), F32)
            for s in range(slots):
                pair = pair_ref[p * slots + s]
                head = pair % heads if blocks > 1 else pair
                start = pl.multiple_of(pair // heads * BLOCK, BLOCK) if blocks > 1 else 0
                lane = pl.multiple_of(head * D_HEAD, D_HEAD)
                k = k_ref[pl.ds(start, BLOCK), pl.ds(lane, D_HEAD)]
                v = v_ref[pl.ds(lane, D_HEAD), pl.ds(start, BLOCK)]
                q = q_ref[i, s * TILE : (s + 1) * TILE, :]
                weights, total, lse = soft(dot_nt(k, q))
                out = jnp.dot(v, weights, preferred_element_type=F32) / total
                out_ref[i, s * TILE : (s + 1) * TILE, :] = out.astype(BF16)
                high = lse.astype(BF16).astype(F32)
                middle = (lse - high).astype(BF16).astype(F32)
                low = lse - high - middle
                logs = jnp.where(sub == 3 * s, high, logs)
                logs = jnp.where(sub == 3 * s + 1, middle, logs)
                logs = jnp.where(sub == 3 * s + 2, low, logs)
            out_ref[i, slots * TILE :, :] = logs.astype(BF16)

    return pl.pallas_call(
        body,
        grid=(peers // group,),
        in_specs=[
            smem(),
            pl.BlockSpec((group, rows, TILE), lambda i: (i, 0, 0)),
            pl.BlockSpec(keys.shape, lambda i: (0, 0)),
            pl.BlockSpec(values_t.shape, lambda i: (0, 0)),
        ],
        out_specs=pl.BlockSpec((group, out_rows, TILE), lambda i: (i, 0, 0)),
        out_shape=jax.ShapeDtypeStruct((peers, out_rows, TILE), BF16),
        name="attend",
    )(pairs, incoming, keys, values_t)


def own_attention(queries, keys, values, prefix_values):
    tok_rows, width = queries.shape
    heads = width // D_HEAD
    blocks = tok_rows // BLOCK

    def body(q_ref, k_ref, v_ref, pv_ref, out_ref, lse_ref, turned_ref):
        turned_ref[...] = pv_ref[...].T
        v_t = v_ref[...].T
        for t in range(BLOCK // TILE):
            seen = (t + 1) * TILE
            scores = dot_nt(k_ref[:seen, :], q_ref[t * TILE : seen, :])
            key = lax.broadcasted_iota(jnp.int32, scores.shape, 0)
            query = lax.broadcasted_iota(jnp.int32, scores.shape, 1) + t * TILE
            weights, total, lse = soft(jnp.where(key <= query, scores, -jnp.inf))
            out = jnp.dot(v_t[:, :seen], weights, preferred_element_type=F32) / total
            out_ref[:, t * TILE : seen] = out
            lse_ref[0, :, t * TILE : seen] = lse

    block = pl.BlockSpec((BLOCK, D_HEAD), lambda b, h: (b, h))
    block_t = pl.BlockSpec((D_HEAD, BLOCK), lambda b, h: (h, b))
    return pl.pallas_call(
        body,
        grid=(blocks, heads),
        in_specs=[block] * 4,
        out_specs=[block_t, pl.BlockSpec((1, 1, BLOCK), lambda b, h: (h, 0, b)), block_t],
        out_shape=[
            jax.ShapeDtypeStruct((width, tok_rows), F32),
            jax.ShapeDtypeStruct((heads, 1, tok_rows), F32),
            jax.ShapeDtypeStruct((width, tok_rows), BF16),
        ],
        name="own",
    )(queries, keys, values, prefix_values)


def combine(owner, rank, place, backs, own_out, own_lse, parts):
    peers = backs[0].shape[0]
    width, tok_rows = own_out.shape
    heads = width // D_HEAD
    tiles = tok_rows // TILE
    chunk = width // peers

    def body(owner_ref, rank_ref, place_ref, *refs):
        back_refs, (out_ref, lse_ref, att_ref, turned) = refs[: len(parts)], refs[len(parts) :]
        t = pl.program_id(0)

        def answer(r):
            p, rank = owner_ref[r], rank_ref[r]
            first, part, log = 0, None, None
            for n, back_ref in zip(parts, back_refs):
                s = jnp.clip(rank - first, 0, n - 1)
                here = back_ref[p, pl.ds(pl.multiple_of(s * TILE, TILE), TILE), :]
                terms = back_ref[p, n * TILE :, :].astype(F32)
                sub = lax.broadcasted_iota(jnp.int32, terms.shape, 0)
                mine = jnp.logical_and(sub >= 3 * s, sub < 3 * s + 3)
                here_log = jnp.sum(jnp.where(mine, terms, 0.0), axis=0, keepdims=True)
                part = here if part is None else jnp.where(rank >= first, here, part)
                log = here_log if log is None else jnp.where(rank >= first, here_log, log)
                first += n
            return part.astype(F32), log

        for h in range(heads):
            logs, pieces = [lse_ref[h]], [out_ref[h * D_HEAD : (h + 1) * D_HEAD, :]]
            for j in range(TOPK):
                piece, log = answer((t * heads + h) * TOPK + j)
                pieces.append(piece)
                logs.append(log)
            top = logs[0]
            for log in logs[1:]:
                top = jnp.maximum(top, log)
            factors = [jnp.exp(log - top) for log in logs]
            total = factors[0]
            for factor in factors[1:]:
                total = total + factor
            inverse = 1.0 / total
            mixed = pieces[0] * (factors[0] * inverse)
            for factor, piece in zip(factors[1:], pieces[1:]):
                mixed = mixed + piece * (factor * inverse)
            for i in range(D_HEAD // chunk):
                at = pl.multiple_of(place_ref[h * (D_HEAD // chunk) + i] * chunk, chunk)
                turned[pl.ds(at, chunk), :] = mixed[i * chunk : (i + 1) * chunk, :]
        for h in range(heads):
            lanes = slice(h * D_HEAD, (h + 1) * D_HEAD)
            att_ref[:, lanes] = turned[lanes, :].T.astype(BF16)

    return pl.pallas_call(
        body,
        grid=(tiles,),
        in_specs=[smem(), smem(), smem()]
        + [pl.BlockSpec(back.shape, lambda i: (0, 0, 0)) for back in backs]
        + [
            pl.BlockSpec((width, TILE), lambda i: (0, i)),
            pl.BlockSpec((heads, 1, TILE), lambda i: (0, 0, i)),
        ],
        out_specs=pl.BlockSpec((TILE, width), lambda i: (i, 0)),
        out_shape=jax.ShapeDtypeStruct((tok_rows, width), BF16),
        scratch_shapes=[pltpu.VMEM((width, TILE), F32)],
        name="combine",
    )(owner, rank, place, *backs, own_out, own_lse)


def project(att_own, att_other, weights):
    rows, depth = att_own.shape
    piece, width = weights[0].shape
    part = min(width, 512)

    def body(a_ref, b_ref, w0, w1, w2, w3, out_ref):
        total = jnp.dot(a_ref[:, :piece], w0[...], preferred_element_type=F32)
        total += jnp.dot(a_ref[:, piece:], w1[...], preferred_element_type=F32)
        total += jnp.dot(b_ref[:, :piece], w2[...], preferred_element_type=F32)
        total += jnp.dot(b_ref[:, piece:], w3[...], preferred_element_type=F32)
        out_ref[...] = total.astype(BF16)

    held = pl.BlockSpec((rows, depth), lambda i: (0, 0))
    weight = pl.BlockSpec((piece, part), lambda i: (0, i))
    return pl.pallas_call(
        body,
        grid=(width // part,),
        in_specs=[held, held] + [weight] * 4,
        out_specs=pl.BlockSpec((rows, part), lambda i: (0, i)),
        out_shape=jax.ShapeDtypeStruct((rows, width), BF16),
        name="project",
    )(att_own, att_other, *weights)


def bit_orders(peers):
    bits = int(math.log2(peers))
    high = list(range(bits - 1, 2, -1))
    return [high + [2, 1, 0], high + [2, 0, 1]]


def doubling_pairs(peers, orders, step, crossed=False):
    pairs = []
    for c in range(peers):
        for h in range(2):
            pairs.append((2 * c + h, 2 * (c ^ (1 << orders[h][step])) + (1 - h if crossed else h)))
    return pairs


def joined(a, b):
    return lax.optimization_barrier(jnp.concatenate([a, b], axis=0))


def shards(queries, keys, values, prefix_keys, prefix_values, selected, out_weight):
    tok_rows, width = queries.shape
    heads = width // D_HEAD
    tiles = tok_rows // TILE
    blocks_here = prefix_keys.shape[0] // BLOCK
    peers = lax.axis_size("ctx")
    me, core = lax.axis_index("ctx"), lax.axis_index("head")
    requests = tiles * heads * TOPK
    capacity = -(-requests // (peers * blocks_here))
    slots = capacity * blocks_here
    swap = [(0, 1), (1, 0)]
    both = ("ctx", "head")

    orders = bit_orders(peers)
    steps = len(orders[0])
    weight = out_weight[0]
    for step in range(steps - 1):
        got = lax.ppermute(weight, both, doubling_pairs(peers, orders, step))
        weight = joined(weight, got)
    half = weight.shape[1] // 2
    mine = lax.dynamic_slice_in_dim(weight, core * half, half, 1)
    theirs = lax.dynamic_slice_in_dim(weight, (1 - core) * half, half, 1)
    mine, theirs = lax.optimization_barrier((mine, theirs))
    far_own = lax.ppermute(mine, both, doubling_pairs(peers, orders, steps - 1))
    far_other = lax.ppermute(theirs, both, doubling_pairs(peers, orders, steps - 1, True))
    near_other = lax.ppermute(theirs, "head", swap)

    parts = [slots]
    outgoing, owner, rank = route_queries(
        selected.reshape(requests), queries, peers, parts, blocks_here
    )
    incoming = []
    for sent in outgoing:
        incoming.append(lax.all_to_all(sent, "ctx", split_axis=0, concat_axis=0, tiled=True))
    own_out, own_lse, turned = own_attention(queries, keys, values, prefix_values)

    apart = jnp.arange(peers, dtype=jnp.int32) ^ me
    places = [sum(((apart >> bit) & 1) << k for k, bit in enumerate(order)) for order in orders]
    place = jnp.where(core == 0, places[0], places[1])

    backs = []
    for n, asked in zip(parts, incoming):
        pairs = asked[:, n * TILE : n * TILE + n, 0].astype(jnp.int32).reshape(peers * n)
        answers = attend_slots(pairs, asked, prefix_keys, turned, n, heads)
        backs.append(lax.all_to_all(answers, "ctx", split_axis=0, concat_axis=0, tiled=True))
    att = combine(owner, rank, place, backs, own_out, own_lse, parts)
    att_other = lax.ppermute(att, "head", swap)
    return project(att, att_other, (mine, far_own, near_other, far_other))


def solution(mesh):
    return jax.shard_map(
        shards,
        mesh=mesh,
        in_specs=(
            P("ctx", "head"),
            P("ctx", "head"),
            P("ctx", "head"),
            P("ctx", "head"),
            P("ctx", "head"),
            P("head", "ctx", None, None),
            P("head", "ctx", None),
        ),
        out_specs=P("ctx", "head"),
        check_vma=False,
    )
```

time: 305 us -> 293 us (0.961)
  local copies, waits for them, and re-layouts: 33.2 us -> 8.03 us
  waiting for transfers between devices: 184 us -> 193 us
    unnamed x29 -> x7, local copies, waits for them, and re-layouts: 23.7 us -> 3.89 us
    ppermute x9 -> x6, waiting for transfers between devices: 124 us -> 132 us  [the longest x3 95.9 us: shards(): got = lax.ppermute(weight, both, doubling_pairs(peers, orders, step))]
    concatenate x2 -> x0, local copies, waits for them, and re-layouts: 6.35 us -> none  [the longest x1 3.22 us: shards(): w_other = jnp.concatenate([w_other, got], axis=0)]
    ppermute x9 -> x6, starting transfers between devices: 10.9 us -> 9.47 us  [the longest x3 7.33 us: shards(): got = lax.ppermute(weight, both, doubling_pairs(peers, orders, step))]
  transfers between devices with their start and end apart: 12 -> 9, of which waited for: 9 -> 5; matrix products, arithmetic and copies ran while one was open for 10% -> 3% of each run, Pallas kernels for 5% -> 12%
where the time goes in v2:
time: 293 us; the launch traced here: 291 us
  waiting for transfers between devices  193 us (66%)
  Pallas kernels  48.9 us (17%)
  starting transfers between devices  35.4 us (12%)
  local copies, waits for them, and re-layouts  8.03 us (3%)
  other arithmetic  6.44 us (2%)
    ppermute x3, waiting for transfers between devices, shards(): got = lax.ppermute(weight, both, doubling_pairs(peers, orders, step))  95.9 us
    all_to_all x1, waiting for transfers between devices, shards(): lax.all_to_all(sent, 'ctx', split_axis=0, concat_axis=0, tiled=True)  60.2 us
    ppermute x1, waiting for transfers between devices, shards(): lax.ppermute(theirs, both, doubling_pairs(peers, orders, steps - 1, True))  21 us
    pallas_call x1, Pallas kernels, attend_slots(): pl.pallas_call(body, grid=(peers // group,), in_specs=[smem(), pl.BlockSp...  19.9 us
    all_to_all x1, starting transfers between devices, shards(): lax.all_to_all(answers, 'ctx', split_axis=0, concat_axis=0, tiled=True)  16.9 us
    ppermute x1, waiting for transfers between devices, shards(): far_own = lax.ppermute(mine, both, doubling_pairs(peers, orders, steps - 1))  15.6 us
    pallas_call x1, Pallas kernels, own_attention(): pl.pallas_call(body, grid=(blocks, heads), in_specs=[block] * 4, out_spec...  10.2 us
    pallas_call x1, Pallas kernels, project(): pl.pallas_call(body, grid=(width // part,), in_specs=[held, held] + [weig...  8.77 us
  transfers between devices with their start and end apart: 9, of which 5 were waited for; matrix products, arithmetic and copies ran while one was open for 3% of the time, Pallas kernels for 12%

profile of v2, /device:TPU:0, one launch (start us, length us, event | category | flops | bytes accessed | tf_op | source)
XLA Modules:
  0.0 291.5 jit_solution(348064693518542312)
XLA Ops:
  0.0 0.8 copy.9
  0.8 0.6 reshape.7.picked_ref
  1.4 4.4 %route.1 = (bf16[16,784,128]{2,1,0:T(8,128)(2,1)}, s32[96]{0:T(128)}, s32[96]{0:T(128)}) custom-call(s32[96]{0:T(128)} %reshape.7.picked_ref, bf16[512,1024]{1,0:T(8,128)(2,1)} %q_ref.3), custom_call_target="tpu_custom_call" | custom-call | tf_op jit(solution)/shard_map/route/pallas_call | solution.py:83
  5.8 8.3 %all-to-all-start = ((bf16[16,784,128]{2,1,0:T(8,128)(2,1)}), bf16[16,784,128]{2,1,0:T(8,128)(2,1)S(1)}, u32[]{:S(2)}, u32[]{:S(2)}) async-start(bf16[16,784,128]{2,1,0:T(8,128)(2,1)} %get-tuple-element.15), calls=%async_computation | async-start | bytes 6422528 | tf_op jit(solution)/shard_map/all_to_all | solution.py:333
  14.1 2.8 collective-permute-start.1
  17.0 10.2 %own.1 = (f32[1024,512]{1,0:T(8,128)}, f32[8,1,512]{2,1,0:T(1,128)}, bf16[1024,512]{1,0:T(8,128)(2,1)}) custom-call(bf16[512,1024]{1,0:T(8,128)(2,1)} %q_ref.3, bf16[512,1024]{1,0:T(8,128)(2,1)} %k_ref.2, bf16[512,1024]{1,0:T(8,128)(2,1)} %v_ref.1, bf16[512,1024]{1,0:T(8,128)(2,1)} %pv_ref.1), custom_call_target="tpu_custom_call" | custom-call | tf_op jit(solution)/shard_map/own/pallas_call | solution.py:178
  27.2 60.2 %all-to-all-done.q_ref = bf16[16,784,128]{2,1,0:T(8,128)(2,1)S(1)} async-done(((bf16[16,784,128]{2,1,0:T(8,128)(2,1)}), bf16[16,784,128]{2,1,0:T(8,128)(2,1)S(1)}, u32[]{:S(2)}, u32[]{:S(2)}) %all-to-all-start) | async-done | bytes 3211296 | tf_op jit(solution)/shard_map/all_to_all | solution.py:333
  87.4 0.3 convert_reduce_fusion
  87.7 0.9 reshape.8.pair_ref
  88.6 0.4 copy-done.1
  89.1 19.9 %attend.1 = bf16[16,800,128]{2,1,0:T(8,128)(2,1)} custom-call(s32[96]{0:T(128)} %reshape.8.pair_ref, bf16[16,784,128]{2,1,0:T(8,128)(2,1)} %copy-done.1, bf16[512,1024]{1,0:T(8,128)(2,1)} %k_ref.3, bf16[1024,512]{1,0:T(8,128)(2,1)} %get-tuple-element.16.v_ref), custom_call_target="tpu_custom_call" | custom-call | tf_op jit(solution)/shard_map/attend/pallas_call | solution.py:143
  109.0 16.9 %all-to-all-start.1 = ((bf16[16,800,128]{2,1,0:T(8,128)(2,1)}), bf16[16,800,128]{2,1,0:T(8,128)(2,1)S(1)}, u32[]{:S(2)}, u32[]{:S(2)}) async-start(bf16[16,800,128]{2,1,0:T(8,128)(2,1)} %attend.1), calls=%async_computation.1 | async-start | bytes 6553600 | tf_op jit(solution)/shard_map/all_to_all | solution.py:344
  125.8 0.0 collective-permute-done.1
  125.9 1.3 pad_maximum_fusion.2
  127.2 2.0 collective-permute-start.2
  129.1 71.5 %collective-permute-done.2 = bf16[128,4096]{1,0:T(8,128)(2,1)S(1)} collective-permute-done((bf16[128,4096]{1,0:T(8,128)(2,1)S(1)}, bf16[128,4096]{1,0:T(8,128)(2,1)S(1)}, u32[]{:S(2)}, u32[]{:S(2)}) %collective-permute-start.2) | collective-permute-done | bytes 1048608 | tf_op jit(solution)/shard_map/ppermute | solution.py:317
  200.7 1.6 pad_maximum_fusion.1
  202.3 2.5 collective-permute-start.3
  204.8 24.3 %collective-permute-done.3 = bf16[256,4096]{1,0:T(8,128)(2,1)} collective-permute-done((bf16[256,4096]{1,0:T(8,128)(2,1)}, bf16[256,4096]{1,0:T(8,128)(2,1)}, u32[]{:S(2)}, u32[]{:S(2)}) %collective-permute-start.3) | collective-permute-done | bytes 2097184 | tf_op jit(solution)/shard_map/ppermute | solution.py:317
  229.1 2.7 pad_maximum_fusion
  231.8 2.6 constant_dynamic-slice_fusion
  234.4 1.0 collective-permute-start.4
  235.4 0.0 collective-permute-start.5
  235.4 1.2 collective-permute-start.6
  236.6 0.5 broadcast_select_fusion.place_ref
  237.1 1.7 copy-done
  238.8 5.7 %combine.1.a_ref = bf16[512,1024]{1,0:T(8,128)(2,1)} custom-call(s32[96]{0:T(128)} %get-tuple-element.13.owner_ref, s32[96]{0:T(128)} %get-tuple-element.14.rank_ref, s32[16]{0:T(128)} %broadcast_select_fusion.place_ref, bf16[16,800,128]{2,1,0:T(8,128)(2,1)} %copy-done, f32[1024,512]{1,0:T(8,128)} %get-tuple-element.17.refs_1_, ...), custom_call_target="tpu_custom_call" | custom-call | tf_op jit(solution)/shard_map/combine/pallas_call | solution.py:242
  244.4 0.7 collective-permute-start
  245.1 15.6 %collective-permute-done.4.w1 = bf16[512,2048]{1,0:T(8,128)(2,1)} collective-permute-done((bf16[512,2048]{1,0:T(8,128)(2,1)}, bf16[512,2048]{1,0:T(8,128)(2,1)}, u32[]{:S(2)}, u32[]{:S(2)}) %collective-permute-start.4) | collective-permute-done | bytes 2097184 | tf_op jit(solution)/shard_map/ppermute | solution.py:323
  260.8 21.0 %collective-permute-done.6.w3 = bf16[512,2048]{1,0:T(8,128)(2,1)} collective-permute-done((bf16[512,2048]{1,0:T(8,128)(2,1)}, bf16[512,2048]{1,0:T(8,128)(2,1)}, u32[]{:S(2)}, u32[]{:S(2)}) %collective-permute-start.6) | collective-permute-done | bytes 2097184 | tf_op jit(solution)/shard_map/ppermute | solution.py:324
  281.7 1.0 copy-done.2
  282.7 8.8 %project.1 = bf16[512,2048]{1,0:T(8,128)(2,1)} custom-call(bf16[512,1024]{1,0:T(8,128)(2,1)} %combine.1.a_ref, bf16[512,1024]{1,0:T(8,128)(2,1)} %copy-done.2, bf16[512,2048]{1,0:T(8,128)(2,1)} %get-tuple-element.19.w0, bf16[512,2048]{1,0:T(8,128)(2,1)} %collective-permute-done.4.w1, bf16[512,2048]{1,0:T(8,128)(2,1)} %collective-permute-done.5.w2, ...), custom_call_target="tpu_custom_call" | custom-call | tf_op jit(solution)/shard_map/project/pallas_call | solution.py:272
  (6 shorter events, 0.0 us)
Async XLA Ops:
  5.8 81.6 %all-to-all-start = ((bf16[16,784,128]{2,1,0:T(8,128)(2,1)}), bf16[16,784,128]{2,1,0:T(8,128)(2,1)S(1)}, u32[]{:S(2)}, u32[]{:S(2)}) async-start(bf16[16,784,128]{2,1,0:T(8,128)(2,1)} %get-tuple-element.15), calls=%async_computation | async-start | bytes 6422528 | tf_op jit(solution)/shard_map/all_to_all | solution.py:333
  14.1 111.7 %collective-permute-start.1 = (bf16[64,4096]{1,0:T(8,128)(2,1)}, bf16[64,4096]{1,0:T(8,128)(2,1)}, u32[]{:S(2)}, u32[]{:S(2)}) collective-permute-start(bf16[64,4096]{1,0:T(8,128)(2,1)} %bitcast.3), channel_id=1, source_target_pairs={{0,16},{1,17},{2,18},{3,19},{4,20},{5,21},{6,22},{7,23},{8,24},{9,... | collective-permute-start | bytes 1572872 | tf_op jit(solution)/shard_map/ppermute | solution.py:317
  87.4 1.7 copy-start.1
  109.0 128.1 %all-to-all-start.1 = ((bf16[16,800,128]{2,1,0:T(8,128)(2,1)}), bf16[16,800,128]{2,1,0:T(8,128)(2,1)S(1)}, u32[]{:S(2)}, u32[]{:S(2)}) async-start(bf16[16,800,128]{2,1,0:T(8,128)(2,1)} %attend.1), calls=%async_computation.1 | async-start | bytes 6553600 | tf_op jit(solution)/shard_map/all_to_all | solution.py:344
  127.2 73.5 %collective-permute-start.2 = (bf16[128,4096]{1,0:T(8,128)(2,1)S(1)}, bf16[128,4096]{1,0:T(8,128)(2,1)S(1)}, u32[]{:S(2)}, u32[]{:S(2)}) collective-permute-start(bf16[128,4096]{1,0:T(8,128)(2,1)S(1)} %pad_maximum_fusion.2), channel_id=1, source_target_pairs={{0,8},{1,9},{2,10},{3,11},{4,12},{5,13},{6,14},{7,15},{8,0},{9,1},... | collective-permute-start | bytes 3145736 | tf_op jit(solution)/shard_map/ppermute | solution.py:317
  202.3 26.8 %collective-permute-start.3 = (bf16[256,4096]{1,0:T(8,128)(2,1)}, bf16[256,4096]{1,0:T(8,128)(2,1)}, u32[]{:S(2)}, u32[]{:S(2)}) collective-permute-start(bf16[256,4096]{1,0:T(8,128)(2,1)} %pad_maximum_fusion.1), channel_id=1, source_target_pairs={{0,4},{1,3},{2,6},{3,1},{4,0},{5,7},{6,2},{7,5},{8,12},{9,11},{10,... | collective-permute-start | bytes 6291464 | tf_op jit(solution)/shard_map/ppermute | solution.py:317
  234.4 26.4 %collective-permute-start.4 = (bf16[512,2048]{1,0:T(8,128)(2,1)}, bf16[512,2048]{1,0:T(8,128)(2,1)}, u32[]{:S(2)}, u32[]{:S(2)}) collective-permute-start(bf16[512,2048]{1,0:T(8,128)(2,1)} %get-tuple-element.19.w0), channel_id=1, source_target_pairs={{0,2},{1,5},{2,0},{3,7},{4,6},{5,1},{6,4},{7,3},{8,10},{9,13},{10,... | collective-permute-start | bytes 6291464 | tf_op jit(solution)/shard_map/ppermute | solution.py:323
  235.4 25.4 %collective-permute-start.5 = (bf16[512,2048]{1,0:T(8,128)(2,1)}, bf16[512,2048]{1,0:T(8,128)(2,1)}, u32[]{:S(2)}, u32[]{:S(2)}) collective-permute-start(bf16[512,2048]{1,0:T(8,128)(2,1)} %get-tuple-element.20), channel_id=1, source_target_pairs={{0,1},{1,0},{2,3},{3,2},{4,5},{5,4},{6,7},{7,6},{8,9},{9,8},{10,11... | collective-permute-start | bytes 6291464 | tf_op jit(solution)/shard_map/ppermute | solution.py:325
  235.4 46.3 %collective-permute-start.6 = (bf16[512,2048]{1,0:T(8,128)(2,1)}, bf16[512,2048]{1,0:T(8,128)(2,1)}, u32[]{:S(2)}, u32[]{:S(2)}) collective-permute-start(bf16[512,2048]{1,0:T(8,128)(2,1)} %get-tuple-element.20), channel_id=1, source_target_pairs={{0,3},{1,4},{2,1},{3,6},{4,7},{5,0},{6,5},{7,2},{8,11},{9,12},{10,... | collective-permute-start | bytes 6291464 | tf_op jit(solution)/shard_map/ppermute | solution.py:324
  237.1 1.7 copy-start
  244.4 37.3 %collective-permute-start = (bf16[512,1024]{1,0:T(8,128)(2,1)}, bf16[512,1024]{1,0:T(8,128)(2,1)S(1)}, u32[]{:S(2)}, u32[]{:S(2)}) collective-permute-start(bf16[512,1024]{1,0:T(8,128)(2,1)} %combine.1.a_ref), channel_id=1, source_target_pairs={{0,1},{1,0},{2,3},{3,2},{4,5},{5,4},{6,7},{7,6},{8,9},{9,8},{10,11... | collective-permute-start | bytes 3145736 | tf_op jit(solution)/shard_map/ppermute | solution.py:346
  281.7 1.0 copy-start.2
